TPU v7x, 256 devices: a whole 4x4x8 slice. The times are simulated.
256 devices in a mesh: rep: 32 (over y_hi, z, core), tp: 8 (over y_lo, x).
Axes of the slice: x: 4, y: 4 (y_hi: 2, y_lo: 2; y = y_hi * 2 + y_lo), z: 8, core: 2. Of those that a mesh axis runs over, the one named last changes fastest.
Arguments:
- queries: bfloat16 [8192, 8192], P('rep', 'tp'), may hold values from -8 to 8
- cand_keys: bfloat16 [8192, 1024], P('rep', 'tp'), may hold values from -6 to 6
- cand_values: bfloat16 [8192, 1024], P('rep', 'tp'), may hold values from -6 to 6
- prefix_kv: bfloat16 [32, 2, 4096, 1024], P('rep', None, None, 'tp'), may hold values from -8 to 8
- owner: int32 [1], replicated, may hold values from 0 to 31
- lengths: int32 [32, 2], P('rep'), may hold values from 1 to 128, as said below
- out_weight: bfloat16 [8192, 4096], P('tp'), may hold values from -2.390625 to 2.390625
Outputs:
- attn_out: bfloat16 [8192, 4096], P(('rep', 'tp'))
Inputs may be any that keep to these rules, and one draw needn't show every extreme that they name: Only the slice of prefix_kv at index owner[0] is read. Candidate c of group g has its real tokens in its first lengths[g, c] slots; the rest are padding.
All inputs are finite; a program needn't handle non-finite values.
Results may differ from a plain program's by a relative error of at most 0.017.
Values may be sent and summed in bfloat16 or wider, within the bound.
No kernel may reach another device: no remote copies, remote signals or barrier semaphores. Data moves between devices by JAX's collectives and lax.ppermute only.
A program may use at most 64 MiB of HBM per device.

v0:
```python
import math
import jax
import jax.numpy as jnp
from jax import lax
from jax.sharding import PartitionSpec as P

QH = 64
KVH = 8
HD = 128
CLEN = 128
NEG = -1e30


def padded_to(lines, count):
    spare = -len(lines) % count
    return jnp.pad(lines, [(0, spare)] + [(0, 0)] * (lines.ndim - 1))


def broadcast_by_parts(shard, axis, root):
    lines = jnp.where(lax.axis_index(axis) == root, shard, jnp.zeros_like(shard)).reshape(
        -1, *shard.shape[1:][-1:]
    )
    padded = padded_to(lines, lax.axis_size(axis))
    own = lax.psum_scatter(padded, axis, scatter_dimension=0, tiled=True)
    return lax.all_gather(own, axis, axis=0, tiled=True)[: len(lines)].reshape(shard.shape)


def split_up(shard, dim, count):
    before, after = (shard.shape[:dim], shard.shape[dim + 1 :])
    return jnp.moveaxis(shard.reshape(*before, count, -1, *after), dim, 0)


def summed_on_arrival(shard, axis, dim):
    count = lax.axis_size(axis)
    tiles = lax.all_to_all(split_up(shard, dim, count), axis, 0, 0, tiled=True)
    return jnp.sum(tiles.astype(jnp.float32), axis=0)


def body(queries, cand_keys, cand_values, prefix_kv, owner, lengths, out_weight):
    row_count = queries.shape[0]
    kv_heads = cand_keys.shape[1] // HD
    head_group = QH // KVH
    cand_count = row_count // CLEN
    score_scale = 1.0 / math.sqrt(HD)
    query_grid = queries.reshape(row_count, kv_heads, head_group, HD)
    cand_queries = queries.reshape(cand_count, CLEN, kv_heads, head_group, HD)
    key_grid = cand_keys.reshape(cand_count, CLEN, kv_heads, HD)
    value_grid = cand_values.reshape(cand_count, CLEN, kv_heads, HD)
    own_scores = (
        jnp.einsum("cikgd,cjkd->kgcij", cand_queries, key_grid, preferred_element_type=jnp.float32)
        * score_scale
    )
    live_mask = jnp.arange(CLEN, dtype=jnp.int32)[None, :] < lengths[0][:, None]
    own_scores = jnp.where(live_mask[None, None, :, None, :], own_scores, NEG)
    own_max = jnp.max(own_scores, -1)
    exponent = jnp.exp(own_scores - own_max[..., None])
    row_total = jnp.sum(exponent, -1).reshape(kv_heads, head_group, row_count)
    weighted = jnp.einsum(
        "kgcij,cjkd->kgcid",
        exponent.astype(jnp.bfloat16),
        value_grid,
        preferred_element_type=jnp.float32,
    )
    weighted = weighted.reshape(kv_heads, head_group, row_count, HD)
    row_max = own_max.reshape(kv_heads, head_group, row_count)

    def absorb(running, block_keys, block_values):
        old_max, old_total, old_weighted = running
        block_width = block_keys.shape[0]
        scores = (
            jnp.einsum(
                "xlpm,vlm->lpxv",
                query_grid,
                block_keys.reshape(block_width, kv_heads, HD),
                preferred_element_type=jnp.float32,
            )
            * score_scale
        )
        new_max = jnp.maximum(old_max, jnp.max(scores, -1))
        factor = jnp.exp(old_max - new_max)
        block_expo = jnp.exp(scores - new_max[..., None])
        new_total = old_total * factor + jnp.sum(block_expo, -1)
        new_weighted = old_weighted * factor[..., None] + jnp.einsum(
            "ipuo,oit->iput",
            block_expo.astype(jnp.bfloat16),
            block_values.reshape(block_width, kv_heads, HD),
            preferred_element_type=jnp.float32,
        )
        return (new_max, new_total, new_weighted)

    prefix_len = prefix_kv.shape[2]
    block_width = min(1024, prefix_len)
    block_count = prefix_len // block_width
    owner_index = owner[0]
    own_prefix = prefix_kv[0]
    arrived = broadcast_by_parts(own_prefix, "rep", owner_index)

    def advance(block_index, running):
        prefix_piece = lax.dynamic_slice_in_dim(arrived, block_index * block_width, block_width, 1)
        return absorb(running, prefix_piece[0], prefix_piece[1])

    row_max, row_total, weighted = lax.fori_loop(
        0, block_count, advance, (row_max, row_total, weighted)
    )
    context = weighted / row_total[..., None]
    context = (
        jnp.transpose(context, (2, 0, 1, 3))
        .reshape(row_count, kv_heads * head_group * HD)
        .astype(jnp.bfloat16)
    )
    summed = summed_on_arrival(
        jnp.dot(context, out_weight, preferred_element_type=jnp.float32).astype(jnp.bfloat16),
        "tp",
        0,
    )
    return summed.astype(jnp.bfloat16)


def solution(mesh):
    in_specs = (
        P("rep", "tp"),
        P("rep", "tp"),
        P("rep", "tp"),
        P("rep", None, None, "tp"),
        P(),
        P("rep", None),
        P("tp", None),
    )
    out_specs = P(("rep", "tp"), None)
    return jax.shard_map(body, mesh=mesh, in_specs=in_specs, out_specs=out_specs, check_vma=False)
```

profile of v0, /device:TPU:1, one launch (start us, length us, event | category | flops | bytes accessed | tf_op | source)
XLA Modules:
  0.0 312.3 jit_solution(9816006664559664985)
XLA Ops:
  6.5 0.0 copy-start
  6.5 0.0 copy-start.3
  6.5 0.0 copy-start.2
  6.5 0.0 reduce-scatter.2.cloned.1.call-start
  7.2 1.5 broadcast_select_fusion
  8.7 0.0 reduce-scatter.2.cloned.1.call-update
  8.8 0.0 all-gather.2.cloned.1.call-start
  8.8 121.0 %reduce-scatter.2.cloned.1.call-done = bf16[256,128]{1,0:T(8,128)(2,1)} async-done(((bf16[8192,128]{1,0:T(8,128)(2,1)}), bf16[256,128]{1,0:T(8,128)(2,1)}) %reduce-scatter.2.cloned.1.call-update) | async-done | bytes 65552 | tf_op jit(solution)/shard_map/reduce_scatter | solution.py:24
  129.8 0.0 all-gather.2.cloned.1.call-update
  129.8 1.2 copy.15
  131.1 1.1 copy.22
  132.2 0.0 copy-done.3
  132.2 0.1 iota_compare_fusion
  132.3 0.0 copy-done
  132.3 0.3 fusion.29
  132.6 0.0 copy-done.2
  132.7 0.4 convolution_bitcast_fusion
  133.0 0.1 copy.14
  133.1 0.3 copy.16
  133.4 0.2 fusion.24
  133.5 82.6 %all-gather.2.cloned.1.call-done = bf16[8192,128]{1,0:T(8,128)(2,1)} async-done(((bf16[256,128]{1,0:T(8,128)(2,1)}), bf16[8192,128]{1,0:T(8,128)(2,1)}) %all-gather.2.cloned.1.call-update) | async-done | bytes 2097168 | tf_op jit(solution)/shard_map/all_gather | solution.py:25
  216.2 51.1 %while.17 = (s32[]{:T(128)}, f32[1,8,256]{2,1,0:T(8,128)S(1)}, f32[1,8,256]{2,1,0:T(8,128)S(1)}, f32[1,8,256,128]{3,2,1,0:T(8,128)S(1)}, bf16[2,4096,128]{2,1,0:...) while((s32[]{:T(128)}, f32[1,8,256]{2,1,0:T(8,128)S(1)}, ...), condition=%wide.region_6.7_spmd, body=%wide.region_3.6_spmd.sunk | while | flops 1091049472 | bytes 61997260 | solution.py:102
  216.2 5.4 %bitcast_reduce_fusion.2 = (f32[8,256]{1,0:T(8,128)S(1)}, f32[1024,256,8]{1,0,2:T(8,128)}) fusion(bf16[256,1,8,128]{3,0,2,1:T(8,128)(2,1)S(1)} %get-tuple-element.213, bf16[2,4096,128]{2,1,0:T(8,128)(2,1)} %get-tuple-element.212, s32[]{:T(128)S(6)} %select_n.37), kind=kOutput, calls=%fused_computation.1.clone.1 | convolution fusion | flops 541063168 | bytes 9183236 | tf_op jit(solution)/shard_map/while/body/eval_jaxpr/xlpm,vlm->lpxv/dot_general | solution.py:71
  221.6 0.0 copy-start.1
  221.6 4.6 %fusion.41 = f32[1,8,256,128]{3,2,1,0:T(8,128)S(1)} fusion(f32[1024,256,8]{1,0,2:T(8,128)} %get-tuple-element.184, f32[8,256]{1,0:T(8,128)S(1)} %bitcast.126, f32[1,8,256,128]{3,2,1,0:T(8,128)S(1)} %get-tuple-element.200, f32[8,256]{1,0:T(8,128)S(1)} %get-tuple-element.185, bf16[2,4096,128]{2,1,0:T(8,128)(2,1)} %get-tuple-element.212, s32[]{:T(128)S(6)} %add.51, ...), kind=kOutput, calls=%fused_computation.10.clone.1 | convolution fusion | flops 543686656 | bytes 10764296 | tf_op jit(solution)/shard_map/while/body/eval_jaxpr/ipuo,oit->iput/dot_general | solution.py:83
  226.2 1.3 copy-done.1
  227.5 1.4 fusion.40
  228.9 5.4 %bitcast_reduce_fusion.2 = (f32[8,256]{1,0:T(8,128)S(1)}, f32[1024,256,8]{1,0,2:T(8,128)}) fusion(bf16[256,1,8,128]{3,0,2,1:T(8,128)(2,1)S(1)} %get-tuple-element.213, bf16[2,4096,128]{2,1,0:T(8,128)(2,1)} %get-tuple-element.212, s32[]{:T(128)S(6)} %select_n.37), kind=kOutput, calls=%fused_computation.1.clone.1 | convolution fusion | flops 541063168 | bytes 9183236 | tf_op jit(solution)/shard_map/while/body/eval_jaxpr/xlpm,vlm->lpxv/dot_general | solution.py:71
  234.4 0.0 copy-start.1
  234.4 4.6 %fusion.41 = f32[1,8,256,128]{3,2,1,0:T(8,128)S(1)} fusion(f32[1024,256,8]{1,0,2:T(8,128)} %get-tuple-element.184, f32[8,256]{1,0:T(8,128)S(1)} %bitcast.126, f32[1,8,256,128]{3,2,1,0:T(8,128)S(1)} %get-tuple-element.200, f32[8,256]{1,0:T(8,128)S(1)} %get-tuple-element.185, bf16[2,4096,128]{2,1,0:T(8,128)(2,1)} %get-tuple-element.212, s32[]{:T(128)S(6)} %add.51, ...), kind=kOutput, calls=%fused_computation.10.clone.1 | convolution fusion | flops 543686656 | bytes 10764296 | tf_op jit(solution)/shard_map/while/body/eval_jaxpr/ipuo,oit->iput/dot_general | solution.py:83
  239.0 1.3 copy-done.1
  240.3 1.4 fusion.40
  241.7 5.4 %bitcast_reduce_fusion.2 = (f32[8,256]{1,0:T(8,128)S(1)}, f32[1024,256,8]{1,0,2:T(8,128)}) fusion(bf16[256,1,8,128]{3,0,2,1:T(8,128)(2,1)S(1)} %get-tuple-element.213, bf16[2,4096,128]{2,1,0:T(8,128)(2,1)} %get-tuple-element.212, s32[]{:T(128)S(6)} %select_n.37), kind=kOutput, calls=%fused_computation.1.clone.1 | convolution fusion | flops 541063168 | bytes 9183236 | tf_op jit(solution)/shard_map/while/body/eval_jaxpr/xlpm,vlm->lpxv/dot_general | solution.py:71
  247.2 0.0 copy-start.1
  247.2 4.6 %fusion.41 = f32[1,8,256,128]{3,2,1,0:T(8,128)S(1)} fusion(f32[1024,256,8]{1,0,2:T(8,128)} %get-tuple-element.184, f32[8,256]{1,0:T(8,128)S(1)} %bitcast.126, f32[1,8,256,128]{3,2,1,0:T(8,128)S(1)} %get-tuple-element.200, f32[8,256]{1,0:T(8,128)S(1)} %get-tuple-element.185, bf16[2,4096,128]{2,1,0:T(8,128)(2,1)} %get-tuple-element.212, s32[]{:T(128)S(6)} %add.51, ...), kind=kOutput, calls=%fused_computation.10.clone.1 | convolution fusion | flops 543686656 | bytes 10764296 | tf_op jit(solution)/shard_map/while/body/eval_jaxpr/ipuo,oit->iput/dot_general | solution.py:83
  251.8 1.3 copy-done.1
  253.1 1.4 fusion.40
  254.5 5.4 %bitcast_reduce_fusion.2 = (f32[8,256]{1,0:T(8,128)S(1)}, f32[1024,256,8]{1,0,2:T(8,128)}) fusion(bf16[256,1,8,128]{3,0,2,1:T(8,128)(2,1)S(1)} %get-tuple-element.213, bf16[2,4096,128]{2,1,0:T(8,128)(2,1)} %get-tuple-element.212, s32[]{:T(128)S(6)} %select_n.37), kind=kOutput, calls=%fused_computation.1.clone.1 | convolution fusion | flops 541063168 | bytes 9183236 | tf_op jit(solution)/shard_map/while/body/eval_jaxpr/xlpm,vlm->lpxv/dot_general | solution.py:71
  259.9 0.0 copy-start.1
  259.9 4.6 %fusion.41 = f32[1,8,256,128]{3,2,1,0:T(8,128)S(1)} fusion(f32[1024,256,8]{1,0,2:T(8,128)} %get-tuple-element.184, f32[8,256]{1,0:T(8,128)S(1)} %bitcast.126, f32[1,8,256,128]{3,2,1,0:T(8,128)S(1)} %get-tuple-element.200, f32[8,256]{1,0:T(8,128)S(1)} %get-tuple-element.185, bf16[2,4096,128]{2,1,0:T(8,128)(2,1)} %get-tuple-element.212, s32[]{:T(128)S(6)} %add.51, ...), kind=kOutput, calls=%fused_computation.10.clone.1 | convolution fusion | flops 543686656 | bytes 10764296 | tf_op jit(solution)/shard_map/while/body/eval_jaxpr/ipuo,oit->iput/dot_general | solution.py:83
  264.6 1.3 copy-done.1
  265.9 1.4 fusion.40
  267.3 0.3 copy.17
  267.6 0.1 divide_convert_fusion
  267.7 5.8 %convolution_convert_fusion = bf16[256,4096]{1,0:T(8,128)(2,1)S(1)} fusion(bf16[256,1024]{0,1:T(8,128)(2,1)S(1)} %bitcast.129, bf16[1024,4096]{1,0:T(8,128)(2,1)} %param.15), kind=kOutput, calls=%fused_computation.22 | convolution fusion | flops 2148532224 | bytes 11010048 | tf_op jit(solution)/shard_map/dot_general | solution.py:112
  273.5 30.9 %all_to_all.5 = bf16[8,32,4096]{2,1,0:T(8,128)(2,1)S(1)} all-to-all(bf16[8,32,4096]{2,1,0:T(8,128)(2,1)S(1)} %bitcast.124), channel_id=1, replica_groups=mesh['rep'=32,'tp'=8] {'tp'}, dimensions={0} | all-to-all | bytes 4194304 | tf_op jit(solution)/shard_map/all_to_all | solution.py:35
  304.4 1.1 reduce_sum.35
  (12 shorter events, 0.1 us)
Async XLA Ops:
  6.5 125.8 %copy-start = (bf16[256,128]{1,0:T(8,128)(2,1)S(1)}, bf16[256,128]{1,0:T(8,128)(2,1)}, u32[]{:S(2)}) copy-start(bf16[256,128]{1,0:T(8,128)(2,1)} %param.10) | copy-start | bytes 196612
  6.5 125.7 %copy-start.3 = (s32[1,2]{1,0:T(1,128)S(1)}, s32[1,2]{1,0:T(1,128)}, u32[]{:S(2)}) copy-start(s32[1,2]{1,0:T(1,128)} %param.14) | copy-start | bytes 28
  6.5 126.1 %copy-start.2 = (bf16[256,128]{1,0:T(8,128)(2,1)S(1)}, bf16[256,128]{1,0:T(8,128)(2,1)}, u32[]{:S(2)}) copy-start(bf16[256,128]{1,0:T(8,128)(2,1)} %param.11) | copy-start | bytes 196612
  6.5 123.3 %reduce-scatter.2.cloned.1.call-start = ((), (), s32[]{:S(2)}) async-start(), calls=%async_computation.2 | async-start | bytes 2162688 | tf_op jit(solution)/shard_map/reduce_scatter | solution.py:24
  8.8 207.4 %all-gather.2.cloned.1.call-start = ((), (), s32[]{:S(2)}) async-start(), calls=%async_computation.3 | async-start | bytes 2162688 | tf_op jit(solution)/shard_map/all_gather | solution.py:25
  221.6 5.9 %copy-start.1 = (f32[1024,256,8]{1,0,2:T(8,128)S(1)}, f32[1024,256,8]{1,0,2:T(8,128)}, u32[]{:S(2)}) copy-start(f32[1024,256,8]{1,0,2:T(8,128)} %get-tuple-element.184) | copy-start | bytes 25165828 | tf_op jit(solution)/shard_map/while
  234.4 5.9 %copy-start.1 = (f32[1024,256,8]{1,0,2:T(8,128)S(1)}, f32[1024,256,8]{1,0,2:T(8,128)}, u32[]{:S(2)}) copy-start(f32[1024,256,8]{1,0,2:T(8,128)} %get-tuple-element.184) | copy-start | bytes 25165828 | tf_op jit(solution)/shard_map/while
  247.2 5.9 %copy-start.1 = (f32[1024,256,8]{1,0,2:T(8,128)S(1)}, f32[1024,256,8]{1,0,2:T(8,128)}, u32[]{:S(2)}) copy-start(f32[1024,256,8]{1,0,2:T(8,128)} %get-tuple-element.184) | copy-start | bytes 25165828 | tf_op jit(solution)/shard_map/while
  259.9 5.9 %copy-start.1 = (f32[1024,256,8]{1,0,2:T(8,128)S(1)}, f32[1024,256,8]{1,0,2:T(8,128)}, u32[]{:S(2)}) copy-start(f32[1024,256,8]{1,0,2:T(8,128)} %get-tuple-element.184) | copy-start | bytes 25165828 | tf_op jit(solution)/shard_map/while
Sparse Core Ops, SparseCore 0:
  11.5 118.2 reduce-scatter.1
  132.6 83.5 all-gather.1
where the time goes:
time: 313 us; the launch traced here: 312 us
  waiting for transfers between devices  204 us (65%)
  matrix products  46.6 us (15%)
  blocking collectives  30.9 us (10%)
  between operations  14.2 us (5%)
  other arithmetic  8.46 us (3%)
  local copies, waits for them, and re-layouts  8.3 us (3%)
    reduce_scatter x1, waiting for transfers between devices, broadcast_by_parts(): own = lax.psum_scatter(padded, axis, scatter_dimension=0, tiled=True)  121 us
    all_gather x1, waiting for transfers between devices, broadcast_by_parts(): lax.all_gather(own, axis, axis=0, tiled=True)[:len(lines)]  82.6 us
    all_to_all x1, blocking collectives, summed_on_arrival(): tiles = lax.all_to_all(split_up(shard, dim, count), axis, 0, 0, tiled=True)  30.9 us
    dot_general x4, matrix products, absorb(): jnp.einsum('xlpm,vlm->lpxv', query_grid, block_keys.reshape(block_width,...  21.7 us
    dot_general x4, matrix products, absorb(): jnp.einsum('ipuo,oit->iput', block_expo.astype(jnp.bfloat16), block_value...  18.4 us
  transfers between devices with their start and end apart: 2, of which 2 were waited for; matrix products, arithmetic and copies ran while one was open for 1% of the time, Pallas kernels for 0%

commit v1 on v0

--- a/solution.py
+++ b/solution.py
@@ -11,6 +11,11 @@
 NEG = -1e30
 
 
+def swapped_in(value, mesh_axis, d):
+    sent = jnp.stack([value] * lax.axis_size(mesh_axis))
+    return jnp.concatenate(lax.all_to_all(sent, mesh_axis, 0, 0), axis=d)
+
+
 def padded_to(lines, count):
     spare = -len(lines) % count
     return jnp.pad(lines, [(0, spare)] + [(0, 0)] * (lines.ndim - 1))
@@ -22,7 +27,7 @@
     )
     padded = padded_to(lines, lax.axis_size(axis))
     own = lax.psum_scatter(padded, axis, scatter_dimension=0, tiled=True)
-    return lax.all_gather(own, axis, axis=0, tiled=True)[: len(lines)].reshape(shard.shape)
+    return swapped_in(own, axis, 0)[: len(lines)].reshape(shard.shape)
 
 
 def split_up(shard, dim, count):

time: 313 us -> 293 us (0.936)
  waiting for transfers between devices: 204 us -> 170 us
  starting transfers between devices: 0.04 us -> 11.8 us
    all_gather x1 -> x0, waiting for transfers between devices: 82.6 us -> none  [broadcast_by_parts(): lax.all_gather(own, axis, axis=0, tiled=True)[:len(lines)]]
    all_to_all x0 -> x1, waiting for transfers between devices: none -> 49.2 us  [swapped_in(): return jnp.concatenate(lax.all_to_all(sent, mesh_axis, 0, 0), axis=d)]
    all_to_all x0 -> x1, starting transfers between devices: none -> 11.7 us  [swapped_in(): return jnp.concatenate(lax.all_to_all(sent, mesh_axis, 0, 0), axis=d)]
where the time goes in v1:
time: 293 us; the launch traced here: 291 us
  waiting for transfers between devices  170 us (58%)
  matrix products  46.6 us (16%)
  blocking collectives  30.4 us (10%)
  between operations  14.2 us (5%)
  starting transfers between devices  11.8 us (4%)
  local copies, waits for them, and re-layouts  8.87 us (3%)
  other arithmetic  8.46 us (3%)
    reduce_scatter x1, waiting for transfers between devices, broadcast_by_parts(): own = lax.psum_scatter(padded, axis, scatter_dimension=0, tiled=True)  121 us
    all_to_all x1, waiting for transfers between devices, swapped_in(): return jnp.concatenate(lax.all_to_all(sent, mesh_axis, 0, 0), axis=d)  49.2 us
    all_to_all x1, blocking collectives, summed_on_arrival(): tiles = lax.all_to_all(split_up(shard, dim, count), axis, 0, 0, tiled=True)  30.4 us
    dot_general x4, matrix products, absorb(): jnp.einsum('xlpm,vlm->lpxv', query_grid, block_keys.reshape(block_width,...  21.7 us
    dot_general x4, matrix products, absorb(): jnp.einsum('ipuo,oit->iput', block_expo.astype(jnp.bfloat16), block_value...  18.4 us
    all_to_all x1, starting transfers between devices, swapped_in(): return jnp.concatenate(lax.all_to_all(sent, mesh_axis, 0, 0), axis=d)  11.7 us
  transfers between devices with their start and end apart: 2, of which 2 were waited for; matrix products, arithmetic and copies ran while one was open for 1% of the time, Pallas kernels for 0%

profile of v1, /device:TPU:1, one launch (start us, length us, event | category | flops | bytes accessed | tf_op | source)
XLA Modules:
  0.0 290.6 jit_solution(16596586488940000652)
XLA Ops:
  6.5 0.0 copy-start
  6.5 0.0 copy-start.2
  6.5 0.0 copy-start.4
  6.5 0.0 copy-start.3
  6.5 0.0 reduce-scatter.2.cloned.1.call-start
  7.3 1.5 broadcast_select_fusion
  8.8 0.0 reduce-scatter.2.cloned.1.call-update
  8.8 121.0 %reduce-scatter.2.cloned.1.call-done = bf16[256,128]{1,0:T(8,128)(2,1)} async-done(((bf16[8192,128]{1,0:T(8,128)(2,1)}), bf16[256,128]{1,0:T(8,128)(2,1)}) %reduce-scatter.2.cloned.1.call-update) | async-done | bytes 65552 | tf_op jit(solution)/shard_map/reduce_scatter | solution.py:29
  129.8 2.7 stack.2
  132.5 11.7 %all-to-all-start = ((bf16[32,256,128]{2,1,0:T(8,128)(2,1)}), bf16[32,256,128]{2,1,0:T(8,128)(2,1)}, u32[]{:S(2)}, u32[]{:S(2)}) async-start(bf16[32,256,128]{2,1,0:T(8,128)(2,1)} %stack.2), calls=%async_computation.1 | async-start | bytes 4194304 | tf_op jit(solution)/shard_map/all_to_all | solution.py:16
  144.2 0.0 copy-done.2
  144.2 0.2 copy.15
  144.4 0.1 copy.22
  144.5 0.0 copy-done.4
  144.6 0.1 iota_compare_fusion
  144.6 0.0 copy-done
  144.6 0.3 fusion.29
  145.0 0.0 copy-done.3
  145.0 0.4 convolution_bitcast_fusion
  145.3 0.1 copy.14
  145.4 0.3 copy.16
  145.7 0.2 fusion.24
  145.9 49.2 %all-to-all-done = bf16[32,256,128]{2,1,0:T(8,128)(2,1)} async-done(((bf16[32,256,128]{2,1,0:T(8,128)(2,1)}), bf16[32,256,128]{2,1,0:T(8,128)(2,1)}, u32[]{:S(2)}, u32[]{:S(2)}) %all-to-all-start) | async-done | bytes 2097184 | tf_op jit(solution)/shard_map/all_to_all | solution.py:16
  195.0 51.1 %while.17 = (s32[]{:T(128)}, f32[1,8,256]{2,1,0:T(8,128)S(1)}, f32[1,8,256]{2,1,0:T(8,128)S(1)}, f32[1,8,256,128]{3,2,1,0:T(8,128)S(1)}, bf16[2,4096,128]{2,1,0:...) while((s32[]{:T(128)}, f32[1,8,256]{2,1,0:T(8,128)S(1)}, ...), condition=%wide.region_6.7_spmd, body=%wide.region_3.6_spmd.sunk | while | flops 1091049472 | bytes 61997260 | solution.py:107
  195.0 5.4 %bitcast_reduce_fusion.2 = (f32[8,256]{1,0:T(8,128)S(1)}, f32[1024,256,8]{1,0,2:T(8,128)}) fusion(bf16[256,1,8,128]{3,0,2,1:T(8,128)(2,1)S(1)} %get-tuple-element.213, bf16[2,4096,128]{2,1,0:T(8,128)(2,1)} %get-tuple-element.212, s32[]{:T(128)S(6)} %select_n.37), kind=kOutput, calls=%fused_computation.1.clone.1 | convolution fusion | flops 541063168 | bytes 9183236 | tf_op jit(solution)/shard_map/while/body/eval_jaxpr/xlpm,vlm->lpxv/dot_general | solution.py:76
  200.5 0.0 copy-start.1
  200.5 4.6 %fusion.41 = f32[1,8,256,128]{3,2,1,0:T(8,128)S(1)} fusion(f32[1024,256,8]{1,0,2:T(8,128)} %get-tuple-element.184, f32[8,256]{1,0:T(8,128)S(1)} %bitcast.126, f32[1,8,256,128]{3,2,1,0:T(8,128)S(1)} %get-tuple-element.200, f32[8,256]{1,0:T(8,128)S(1)} %get-tuple-element.185, bf16[2,4096,128]{2,1,0:T(8,128)(2,1)} %get-tuple-element.212, s32[]{:T(128)S(6)} %add.51, ...), kind=kOutput, calls=%fused_computation.10.clone.1 | convolution fusion | flops 543686656 | bytes 10764296 | tf_op jit(solution)/shard_map/while/body/eval_jaxpr/ipuo,oit->iput/dot_general | solution.py:88
  205.1 1.3 copy-done.1
  206.4 1.4 fusion.40
  207.8 5.4 %bitcast_reduce_fusion.2 = (f32[8,256]{1,0:T(8,128)S(1)}, f32[1024,256,8]{1,0,2:T(8,128)}) fusion(bf16[256,1,8,128]{3,0,2,1:T(8,128)(2,1)S(1)} %get-tuple-element.213, bf16[2,4096,128]{2,1,0:T(8,128)(2,1)} %get-tuple-element.212, s32[]{:T(128)S(6)} %select_n.37), kind=kOutput, calls=%fused_computation.1.clone.1 | convolution fusion | flops 541063168 | bytes 9183236 | tf_op jit(solution)/shard_map/while/body/eval_jaxpr/xlpm,vlm->lpxv/dot_general | solution.py:76
  213.3 0.0 copy-start.1
  213.3 4.6 %fusion.41 = f32[1,8,256,128]{3,2,1,0:T(8,128)S(1)} fusion(f32[1024,256,8]{1,0,2:T(8,128)} %get-tuple-element.184, f32[8,256]{1,0:T(8,128)S(1)} %bitcast.126, f32[1,8,256,128]{3,2,1,0:T(8,128)S(1)} %get-tuple-element.200, f32[8,256]{1,0:T(8,128)S(1)} %get-tuple-element.185, bf16[2,4096,128]{2,1,0:T(8,128)(2,1)} %get-tuple-element.212, s32[]{:T(128)S(6)} %add.51, ...), kind=kOutput, calls=%fused_computation.10.clone.1 | convolution fusion | flops 543686656 | bytes 10764296 | tf_op jit(solution)/shard_map/while/body/eval_jaxpr/ipuo,oit->iput/dot_general | solution.py:88
  217.9 1.3 copy-done.1
  219.2 1.4 fusion.40
  220.6 5.4 %bitcast_reduce_fusion.2 = (f32[8,256]{1,0:T(8,128)S(1)}, f32[1024,256,8]{1,0,2:T(8,128)}) fusion(bf16[256,1,8,128]{3,0,2,1:T(8,128)(2,1)S(1)} %get-tuple-element.213, bf16[2,4096,128]{2,1,0:T(8,128)(2,1)} %get-tuple-element.212, s32[]{:T(128)S(6)} %select_n.37), kind=kOutput, calls=%fused_computation.1.clone.1 | convolution fusion | flops 541063168 | bytes 9183236 | tf_op jit(solution)/shard_map/while/body/eval_jaxpr/xlpm,vlm->lpxv/dot_general | solution.py:76
  226.0 0.0 copy-start.1
  226.0 4.6 %fusion.41 = f32[1,8,256,128]{3,2,1,0:T(8,128)S(1)} fusion(f32[1024,256,8]{1,0,2:T(8,128)} %get-tuple-element.184, f32[8,256]{1,0:T(8,128)S(1)} %bitcast.126, f32[1,8,256,128]{3,2,1,0:T(8,128)S(1)} %get-tuple-element.200, f32[8,256]{1,0:T(8,128)S(1)} %get-tuple-element.185, bf16[2,4096,128]{2,1,0:T(8,128)(2,1)} %get-tuple-element.212, s32[]{:T(128)S(6)} %add.51, ...), kind=kOutput, calls=%fused_computation.10.clone.1 | convolution fusion | flops 543686656 | bytes 10764296 | tf_op jit(solution)/shard_map/while/body/eval_jaxpr/ipuo,oit->iput/dot_general | solution.py:88
  230.7 1.3 copy-done.1
  232.0 1.4 fusion.40
  233.4 5.4 %bitcast_reduce_fusion.2 = (f32[8,256]{1,0:T(8,128)S(1)}, f32[1024,256,8]{1,0,2:T(8,128)}) fusion(bf16[256,1,8,128]{3,0,2,1:T(8,128)(2,1)S(1)} %get-tuple-element.213, bf16[2,4096,128]{2,1,0:T(8,128)(2,1)} %get-tuple-element.212, s32[]{:T(128)S(6)} %select_n.37), kind=kOutput, calls=%fused_computation.1.clone.1 | convolution fusion | flops 541063168 | bytes 9183236 | tf_op jit(solution)/shard_map/while/body/eval_jaxpr/xlpm,vlm->lpxv/dot_general | solution.py:76
  238.8 0.0 copy-start.1
  238.8 4.6 %fusion.41 = f32[1,8,256,128]{3,2,1,0:T(8,128)S(1)} fusion(f32[1024,256,8]{1,0,2:T(8,128)} %get-tuple-element.184, f32[8,256]{1,0:T(8,128)S(1)} %bitcast.126, f32[1,8,256,128]{3,2,1,0:T(8,128)S(1)} %get-tuple-element.200, f32[8,256]{1,0:T(8,128)S(1)} %get-tuple-element.185, bf16[2,4096,128]{2,1,0:T(8,128)(2,1)} %get-tuple-element.212, s32[]{:T(128)S(6)} %add.51, ...), kind=kOutput, calls=%fused_computation.10.clone.1 | convolution fusion | flops 543686656 | bytes 10764296 | tf_op jit(solution)/shard_map/while/body/eval_jaxpr/ipuo,oit->iput/dot_general | solution.py:88
  243.4 1.3 copy-done.1
  244.7 1.4 fusion.40
  246.2 0.3 copy.17
  246.5 0.1 divide_convert_fusion
  246.6 5.8 %convolution_convert_fusion = bf16[256,4096]{1,0:T(8,128)(2,1)S(1)} fusion(bf16[256,1024]{0,1:T(8,128)(2,1)S(1)} %bitcast.128, bf16[1024,4096]{1,0:T(8,128)(2,1)} %param.15), kind=kOutput, calls=%fused_computation.22 | convolution fusion | flops 2148532224 | bytes 11010048 | tf_op jit(solution)/shard_map/dot_general | solution.py:117
  252.4 30.4 %all_to_all.10 = bf16[8,32,4096]{2,1,0:T(8,128)(2,1)S(1)} all-to-all(bf16[8,32,4096]{2,1,0:T(8,128)(2,1)S(1)} %bitcast.124), channel_id=1, replica_groups=mesh['rep'=32,'tp'=8] {'tp'}, dimensions={0} | all-to-all | bytes 4194304 | tf_op jit(solution)/shard_map/all_to_all | solution.py:40
  282.7 1.1 reduce_sum.35
  (12 shorter events, 0.1 us)
Async XLA Ops:
  6.5 138.1 %copy-start = (bf16[256,128]{1,0:T(8,128)(2,1)S(1)}, bf16[256,128]{1,0:T(8,128)(2,1)}, u32[]{:S(2)}) copy-start(bf16[256,128]{1,0:T(8,128)(2,1)} %param.10) | copy-start | bytes 196612
  6.5 137.7 %copy-start.2 = (bf16[256,1024]{1,0:T(8,128)(2,1)S(1)}, bf16[256,1024]{1,0:T(8,128)(2,1)}, u32[]{:S(2)}) copy-start(bf16[256,1024]{1,0:T(8,128)(2,1)} %param.9) | copy-start | bytes 1572868
  6.5 138.0 %copy-start.4 = (s32[1,2]{1,0:T(1,128)S(1)}, s32[1,2]{1,0:T(1,128)}, u32[]{:S(2)}) copy-start(s32[1,2]{1,0:T(1,128)} %param.14) | copy-start | bytes 28
  6.5 138.4 %copy-start.3 = (bf16[256,128]{1,0:T(8,128)(2,1)S(1)}, bf16[256,128]{1,0:T(8,128)(2,1)}, u32[]{:S(2)}) copy-start(bf16[256,128]{1,0:T(8,128)(2,1)} %param.11) | copy-start | bytes 196612
  6.5 123.3 %reduce-scatter.2.cloned.1.call-start = ((), (), s32[]{:S(2)}) async-start(), calls=%async_computation.3 | async-start | bytes 2162688 | tf_op jit(solution)/shard_map/reduce_scatter | solution.py:29
  132.5 62.6 %all-to-all-start = ((bf16[32,256,128]{2,1,0:T(8,128)(2,1)}), bf16[32,256,128]{2,1,0:T(8,128)(2,1)}, u32[]{:S(2)}, u32[]{:S(2)}) async-start(bf16[32,256,128]{2,1,0:T(8,128)(2,1)} %stack.2), calls=%async_computation.1 | async-start | bytes 4194304 | tf_op jit(solution)/shard_map/all_to_all | solution.py:16
  200.5 5.9 %copy-start.1 = (f32[1024,256,8]{1,0,2:T(8,128)S(1)}, f32[1024,256,8]{1,0,2:T(8,128)}, u32[]{:S(2)}) copy-start(f32[1024,256,8]{1,0,2:T(8,128)} %get-tuple-element.184) | copy-start | bytes 25165828 | tf_op jit(solution)/shard_map/while
  213.3 5.9 %copy-start.1 = (f32[1024,256,8]{1,0,2:T(8,128)S(1)}, f32[1024,256,8]{1,0,2:T(8,128)}, u32[]{:S(2)}) copy-start(f32[1024,256,8]{1,0,2:T(8,128)} %get-tuple-element.184) | copy-start | bytes 25165828 | tf_op jit(solution)/shard_map/while
  226.0 5.9 %copy-start.1 = (f32[1024,256,8]{1,0,2:T(8,128)S(1)}, f32[1024,256,8]{1,0,2:T(8,128)}, u32[]{:S(2)}) copy-start(f32[1024,256,8]{1,0,2:T(8,128)} %get-tuple-element.184) | copy-start | bytes 25165828 | tf_op jit(solution)/shard_map/while
  238.8 5.9 %copy-start.1 = (f32[1024,256,8]{1,0,2:T(8,128)S(1)}, f32[1024,256,8]{1,0,2:T(8,128)}, u32[]{:S(2)}) copy-start(f32[1024,256,8]{1,0,2:T(8,128)} %get-tuple-element.184) | copy-start | bytes 25165828 | tf_op jit(solution)/shard_map/while
Sparse Core Ops, SparseCore 0:
  11.5 118.2 reduce-scatter.1
